TPU v7x, 32 devices: a whole 2x2x4 slice. The times are simulated.
32 devices in a mesh: grp: 2 (over y), seq: 4 (over z), head: 2 (over x), batch: 2 (over core).
Axes of the slice: x: 2, y: 2, z: 4, core: 2. Of those that a mesh axis runs over, the one named last changes fastest.
Arguments:
- queries: bfloat16 [64, 64, 128], P(('grp', 'batch'), 'head'), parts along dimension 0, may hold values from -8 to 8
- key_cache: bfloat16 [64, 8, 1024, 128], P(('grp', 'batch'), 'head', 'seq'), parts along dimension 0, may hold values from -5 to 5
- value_cache: bfloat16 [64, 8, 1024, 128], P(('grp', 'batch'), 'head', 'seq'), parts along dimension 0, may hold values from -5 to 5
- gate_logits: float32 [2, 64, 64], P(None, ('grp', 'batch'), 'head'), parts along dimension 1, may hold values from -6 to 6
- lengths: int32 [64], P(('grp', 'batch')), parts along dimension 0, may hold values from 256 to 1024, as said below
- chosen: int32 [64, 8, 2], P(('grp', 'batch'), 'head'), parts along dimension 0, may hold values from 0 to 7, as said below
- counts: int32 [64, 8], P(('grp', 'batch'), 'head'), parts along dimension 0, may hold values from 1 to 2, as said below
Outputs:
- output: bfloat16 [64, 64, 128], P(('grp', 'batch'), 'head'), parts along dimension 0
There are 2 independent parts, one for each index of `grp`. A program takes and returns all parts, laid end to end along the dimension named above; each array names one. Nothing has to cross between parts.
Inputs may be any that keep to these rules, and one draw needn't show every extreme that they name: `lengths`: every draw has a sequence of the full length 1024. `chosen`: for each sequence and key-value head the first counts entries are distinct blocks that start below the sequence's length, and the first entry is block 0; the entries after them are ignored. `counts`: every draw has a sequence with 2 valid entries for every key-value head.
All inputs are finite; a program needn't handle non-finite values.
Results may differ from a plain program's by a relative error of at most 0.02.
Values may be sent and summed in bfloat16 or wider, within the bound.
A program may use at most 64 MiB of HBM per device.

v0:
```python
import math

import jax
import jax.numpy as jnp
from jax import lax
from jax.sharding import PartitionSpec as P

BLOCK = 128


def combined_all(array, axis, join):
    gathered = jax.tree.map(
        lambda a, kind: lax.all_gather(a.astype(kind), axis),
        array,
        (jnp.bfloat16, jnp.bfloat16, jnp.bfloat16),
    )

    def take(source):
        return jax.tree.map(
            lambda a, own: lax.dynamic_index_in_dim(a, source, 0, False).astype(own.dtype),
            gathered,
            array,
        )

    return lax.fori_loop(
        1, lax.axis_size(axis), lambda source, state: join(state, take(source)), take(0)
    )


def softmax_terms(query_rows, key_rows, value_rows, live_mask, score_scale):
    scores = (
        jnp.einsum("pgd,pnd->pgn", query_rows, key_rows, preferred_element_type=jnp.float32)
        * score_scale
    )
    scores = jnp.where(live_mask[:, None, :], scores, -1e30)
    row_max = jnp.max(scores, axis=2)
    weights = jnp.where(live_mask[:, None, :], jnp.exp(scores - row_max[:, :, None]), 0.0)
    weight_sum = jnp.sum(weights, axis=2)
    summed = jnp.einsum(
        "pgn,pnd->pgd", weights.astype(jnp.bfloat16), value_rows, preferred_element_type=jnp.float32
    )
    return (row_max, weight_sum, summed)


def combine(first, second):
    merged = []
    for index in range(0, len(first), 3):
        row_max = jnp.maximum(first[index], second[index])
        factor_first = jnp.exp(first[index] - row_max)
        factor_second = jnp.exp(second[index] - row_max)
        merged.append(row_max)
        merged.append(first[index + 1] * factor_first + second[index + 1] * factor_second)
        merged.append(
            first[index + 2] * factor_first[:, :, None]
            + second[index + 2] * factor_second[:, :, None]
        )
    return tuple(merged)


def finish(weight_sum, summed):
    return summed / weight_sum[:, :, None]


def pool_blocks(key_rows, value_rows, pair_lengths, first_block):
    pair_count, tokens, head_width = key_rows.shape
    block_count = tokens // BLOCK
    position = first_block * BLOCK + jnp.arange(tokens, dtype=jnp.int32)
    live_mask = position[None, :] < pair_lengths[:, None]
    token_ones = live_mask.astype(jnp.bfloat16).reshape(pair_count, block_count, BLOCK)
    starts = (first_block + jnp.arange(block_count, dtype=jnp.int32)) * BLOCK
    filled = jnp.clip(pair_lengths[:, None] - starts[None, :], 0, BLOCK)
    root_fill = jnp.sqrt(jnp.maximum(filled, 1).astype(jnp.float32))[:, :, None]
    key_sums = jnp.einsum(
        "pjt,pjtd->pjd",
        token_ones,
        key_rows.reshape(pair_count, block_count, BLOCK, head_width),
        preferred_element_type=jnp.float32,
    )
    value_sums = jnp.einsum(
        "pjt,pjtd->pjd",
        token_ones,
        value_rows.reshape(pair_count, block_count, BLOCK, head_width),
        preferred_element_type=jnp.float32,
    )
    pooled_keys = (key_sums / root_fill).astype(jnp.bfloat16)
    pooled_values = (value_sums / root_fill).astype(jnp.bfloat16)
    return (live_mask, filled > 0, pooled_keys, pooled_values)


def picked_tokens(live_mask, chosen_rows, count_rows, first_block):
    pair_count, tokens = live_mask.shape
    block_count = tokens // BLOCK
    block_ids = first_block + jnp.arange(block_count, dtype=jnp.int32)
    slot_live = jnp.arange(chosen_rows.shape[1], dtype=jnp.int32)[None, :] < count_rows[:, None]
    picked = jnp.any(
        (chosen_rows[:, :, None] == block_ids[None, None, :]) & slot_live[:, :, None], axis=1
    )
    spread = jnp.broadcast_to(picked[:, :, None], (pair_count, block_count, BLOCK)).reshape(
        pair_count, tokens
    )
    return live_mask & spread


def blend_gates(compressed, selected, gate_pairs):
    mixed = gate_pairs[0][:, :, None] * compressed + gate_pairs[1][:, :, None] * selected
    return mixed.astype(jnp.bfloat16)


def on_device(queries, key_cache, value_cache, gate_logits, lengths, chosen, counts):
    batch_rows, head_count, context, head_width = key_cache.shape
    pair_count = batch_rows * head_count
    group_size = queries.shape[1] // head_count
    score_scale = 1.0 / math.sqrt(head_width)
    query_rows = queries.reshape(pair_count, group_size, head_width)
    pair_keys = key_cache.reshape(pair_count, context, head_width)
    pair_values = value_cache.reshape(pair_count, context, head_width)
    pair_lengths = jnp.broadcast_to(lengths[:, None], (batch_rows, head_count)).reshape(pair_count)
    pair_chosen = chosen.reshape(pair_count, chosen.shape[2])
    pair_counts = counts.reshape(pair_count)
    gate_pairs = jax.nn.sigmoid(gate_logits.reshape(2, pair_count, group_size))
    local_blocks = context // BLOCK
    first_block = lax.axis_index("seq") * local_blocks
    live_mask, block_live, pooled_keys, pooled_values = pool_blocks(
        pair_keys, pair_values, pair_lengths, first_block
    )
    token_mask = picked_tokens(live_mask, pair_chosen, pair_counts, first_block)
    all_keys, all_values = (
        lax.all_gather(pooled_keys, "seq", axis=1, tiled=True),
        lax.all_gather(pooled_values, "seq", axis=1, tiled=True),
    )
    all_starts = jnp.arange(all_keys.shape[1], dtype=jnp.int32) * BLOCK
    all_live = all_starts[None, :] < pair_lengths[:, None]
    s_max, s_sum, s_val = softmax_terms(query_rows, pair_keys, pair_values, token_mask, score_scale)
    merged = combined_all((s_max, s_sum, s_val), "seq", combine)
    c_max, c_sum, c_val = softmax_terms(query_rows, all_keys, all_values, all_live, score_scale)
    output = blend_gates(finish(c_sum, c_val), finish(merged[1], merged[2]), gate_pairs)
    return output.reshape(batch_rows, head_count * group_size, head_width)


def solution(mesh):
    return jax.shard_map(
        on_device,
        mesh=mesh,
        in_specs=(
            P(("grp", "batch"), "head", None),
            P(("grp", "batch"), "head", "seq", None),
            P(("grp", "batch"), "head", "seq", None),
            P(None, ("grp", "batch"), "head"),
            P(("grp", "batch")),
            P(("grp", "batch"), "head", None),
            P(("grp", "batch"), "head"),
        ),
        out_specs=P(("grp", "batch"), "head", None),
        check_vma=False,
    )
```

profile of v0, /device:TPU:0, one launch (start us, length us, event | category | flops | bytes accessed | tf_op | source)
XLA Modules:
  0.0 87.3 jit_solution(7308756827463599597)
XLA Ops:
  0.0 0.9 %copy-done = bf16[16,32,128]{2,1,0:T(8,128)(2,1)S(1)} copy-done((bf16[16,32,128]{2,1,0:T(8,128)(2,1)S(1)}, bf16[16,32,128]{2,1,0:T(8,128)(2,1)}, u32[]{:S(2)}) %copy-start) | copy-done | bytes 131096
  0.9 0.7 broadcast_in_dim.71
  1.6 0.1 lt.87
  1.7 0.1 compare_bitcast_fusion
  1.9 3.4 %fusion.17 = f32[64,2,1,128]{3,2,1,0:T(1,128)S(1)} fusion(bf16[64,2,128,128]{3,2,1,0:T(8,128)(2,1)} %bitcast.70, pred[64,2,128,1]{2,1,0,3:T(4,128)(4,1)S(1)} %compare_bitcast_fusion), kind=kOutput, calls=%fused_computation.25 | convolution fusion | flops 4194304 | bytes 4276224 | tf_op jit(solution)/shard_map/pjt,pjtd->pjd/dot_general | solution.py:79
  5.4 3.4 %fusion.19 = f32[64,2,1,128]{3,2,1,0:T(1,128)S(1)} fusion(bf16[64,2,128,128]{3,2,1,0:T(8,128)(2,1)} %bitcast.68, pred[64,2,128,1]{2,1,0,3:T(4,128)(4,1)S(1)} %compare_bitcast_fusion), kind=kOutput, calls=%fused_computation.27 | convolution fusion | flops 4194304 | bytes 4276224 | tf_op jit(solution)/shard_map/pjt,pjtd->pjd/dot_general | solution.py:73
  8.8 0.1 fusion.24
  8.9 15.1 %all_gather.20 = bf16[64,8,128]{2,0,1:T(8,128)(2,1)S(1)} all-gather(bf16[64,2,128]{2,0,1:T(8,128)(2,1)S(1)} %get-tuple-element.207), channel_id=1, replica_groups=mesh['grp'=2,'seq'=4,'head'=2,'batch'=2] {'seq'}, dimensions={1}, use_global_device_ids=true | all-gather | bytes 163840 | tf_op jit(solution)/shard_map/all_gather | solution.py:128
  24.0 0.2 fusion.22
  24.2 0.1 copy.61
  24.4 0.1 copy.62
  24.7 0.1 lt.97
  24.8 0.1 copy.65
  24.9 0.1 eq.15
  25.0 0.1 and_reduce_fusion
  25.1 0.1 copy.67
  25.2 0.1 broadcast_in_dim.76
  25.4 3.5 %fusion.38 = (f32[64,8]{1,0:T(8,128)S(1)}, f32[64,8,256]{2,1,0:T(8,128)S(1)}) fusion(bf16[64,8,128]{2,1,0:T(8,128)(2,1)S(1)} %bitcast.67, bf16[64,256,128]{2,1,0:T(8,128)(2,1)} %bitcast.69, pred[64,256]{1,0:T(8,128)(4,1)S(1)} %bitcast_and_fusion), kind=kOutput, calls=%fused_computation.66 | convolution fusion | flops 33947136 | bytes 4868096 | tf_op jit(solution)/shard_map/pgd,pnd->pgn/dot_general | solution.py:32
  29.0 11.9 %all-gather.3 = bf16[4,64,8]{1,2,0:T(8,128)(2,1)S(1)} all-gather(bf16[1,64,8]{1,2,0:T(8,128)(2,1)S(1)} %copy.68), channel_id=2, replica_groups=mesh['grp'=2,'seq'=4,'head'=2,'batch'=2] {'seq'}, dimensions={0}, use_global_device_ids=true | all-gather | bytes 5120 | tf_op jit(solution)/shard_map/all_gather | solution.py:13
  40.9 0.3 fusion.12
  41.2 11.9 %all-gather.4 = bf16[4,64,8]{1,2,0:T(8,128)(2,1)S(1)} all-gather(bf16[1,64,8]{1,2,0:T(8,128)(2,1)S(1)} %copy.69), channel_id=3, replica_groups=mesh['grp'=2,'seq'=4,'head'=2,'batch'=2] {'seq'}, dimensions={0}, use_global_device_ids=true | all-gather | bytes 5120 | tf_op jit(solution)/shard_map/all_gather | solution.py:13
  53.2 2.9 %convolution_convert_fusion = bf16[64,8,128]{2,1,0:T(8,128)(2,1)S(1)} fusion(bf16[64,256,128]{2,1,0:T(8,128)(2,1)} %bitcast.71, f32[64,8,256]{2,1,0:T(8,128)S(1)} %get-tuple-element.210, f32[64,8]{1,0:T(8,128)S(1)} %get-tuple-element.209, pred[64,256]{1,0:T(8,128)(4,1)S(1)} %bitcast_and_fusion), kind=kOutput, calls=%fused_computation.15 | convolution fusion | flops 34013184 | bytes 4868096 | tf_op jit(solution)/shard_map/pgn,pnd->pgd/dot_general | solution.py:39
  56.1 15.0 %all-gather.2 = bf16[256,8,128]{2,1,0:T(8,128)(2,1)S(1)} all-gather(bf16[64,8,128]{2,1,0:T(8,128)(2,1)S(1)} %convolution_convert_fusion), channel_id=4, replica_groups=mesh['grp'=2,'seq'=4,'head'=2,'batch'=2] {'seq'}, dimensions={0}, use_global_device_ids=true | all-gather | bytes 655360 | tf_op jit(solution)/shard_map/all_gather | solution.py:13
  71.1 1.5 %while.19 = (s32[]{:T(128)}, f32[64,8]{0,1:T(8,128)S(1)}, f32[64,8]{0,1:T(8,128)S(1)}, f32[64,8,128]{2,1,0:T(8,128)S(1)}, bf16[4,64,8]{1,2,0:T(8,128)(2,1)S(1)},...) while((s32[]{:T(128)}, f32[64,8]{0,1:T(8,128)S(1)}, ...), condition=%wide.region_6.7_spmd, body=%wide.region_5.6_spmd.sunk | while | flops 266245 | bytes 682135 | solution.py:25
  71.2 0.1 copy.88
  71.3 0.3 fusion.49
  71.7 0.1 copy.88
  71.8 0.3 fusion.49
  72.2 0.1 copy.88
  72.3 0.3 fusion.49
  72.6 13.3 %all_gather.21 = bf16[64,8,128]{2,0,1:T(8,128)(2,1)S(1)} all-gather(bf16[64,2,128]{2,0,1:T(8,128)(2,1)S(1)} %get-tuple-element.206), channel_id=1, replica_groups=mesh['grp'=2,'seq'=4,'head'=2,'batch'=2] {'seq'}, dimensions={1}, use_global_device_ids=true | all-gather | bytes 163840 | tf_op jit(solution)/shard_map/all_gather | solution.py:129
  86.3 1.0 %fusion.7 = bf16[64,8,128]{2,1,0:T(8,128)(2,1)} fusion(bf16[64,8,8]{2,1,0:T(8,128)(2,1)S(1)} %copy.62, f32[64,8,128]{2,1,0:T(8,128)S(1)} %get-tuple-element.182, bf16[64,8,128]{2,0,1:T(8,128)(2,1)S(1)} %all_gather.21, f32[64,8]{1,0:T(8,128)S(1)} %copy.70, f32[64,8]{1,0:T(8,128)S(1)} %mul.134, f32[64,8]{1,0:T(8,128)S(1)} %copy.64, f32[64,8]{1,0:T(8,128)S(1)} %mul.125), kind=kOutput, calls=%fused_computation.14 | convolution fusion | flops 1441792 | bytes 540672 | tf_op jit(solution)/shard_map/pgn,pnd->pgd/dot_general | solution.py:39
  (35 shorter events, 1.2 us)
Async XLA Ops:
  0.0 0.9 %copy-start = (bf16[16,32,128]{2,1,0:T(8,128)(2,1)S(1)}, bf16[16,32,128]{2,1,0:T(8,128)(2,1)}, u32[]{:S(2)}) copy-start(bf16[16,32,128]{2,1,0:T(8,128)(2,1)} %param.9) | copy-start | bytes 393220
  1.9 22.7 %copy-start.3 = (s32[16,4]{0,1:T(4,128)S(1)}, s32[16,4]{0,1:T(4,128)}, u32[]{:S(2)}) copy-start(s32[16,4]{0,1:T(4,128)} %param.15) | copy-start | bytes 772
  1.9 22.9 %copy-start.2 = (s32[16,4,2]{0,2,1:T(2,128)S(1)}, s32[16,4,2]{0,2,1:T(2,128)}, u32[]{:S(2)}) copy-start(s32[16,4,2]{0,2,1:T(2,128)} %param.14) | copy-start | bytes 1540
  53.2 32.9 %copy-start.1 = (f32[2,16,32]{2,1,0:T(8,128)S(1)}, f32[2,16,32]{2,1,0:T(8,128)}, u32[]{:S(2)}) copy-start(f32[2,16,32]{2,1,0:T(8,128)} %param.12) | copy-start | bytes 12292
where the time goes:
time: 87.6 us; the launch traced here: 87.3 us
  blocking collectives  67.3 us (77%)
  matrix products  14.3 us (16%)
  local copies, waits for them, and re-layouts  3.58 us (4%)
  other arithmetic  1.83 us (2%)
    all_gather x3, blocking collectives, combined_all(): lax.all_gather(a.astype(kind), axis)  38.9 us
    all_gather x1, blocking collectives, on_device(): lax.all_gather(pooled_keys, 'seq', axis=1, tiled=True)  15.1 us
    all_gather x1, blocking collectives, on_device(): lax.all_gather(pooled_values, 'seq', axis=1, tiled=True)  13.3 us
    dot_general x2, matrix products, softmax_terms(): jnp.einsum('pgn,pnd->pgd', weights.astype(jnp.bfloat16), value_rows, pref...  3.93 us
    dot_general x2, matrix products, softmax_terms(): jnp.einsum('pgd,pnd->pgn', query_rows, key_rows, preferred_element_type=j...  3.65 us
    dot_general x1, matrix products, pool_blocks(): jnp.einsum('pjt,pjtd->pjd', token_ones, key_rows.reshape(pair_count, bloc...  3.39 us
    dot_general x1, matrix products, pool_blocks(): jnp.einsum('pjt,pjtd->pjd', token_ones, value_rows.reshape(pair_count, bl...  3.38 us

commit v1 on v0

v1 whole, which is shorter than its diff:
```python
import functools
import math

import jax
import jax.numpy as jnp
from jax import lax
from jax.experimental import pallas as pl
from jax.experimental.pallas import tpu as pltpu
from jax.sharding import PartitionSpec as P

BLOCK = 128
LANES = 128
ROWS = 8
NEG = -1e30
MESH = pl.DeviceIdType.MESH


def kernel(
    n, q_ref, k_hbm, v_hbm, gate_ref, len_ref, chosen_ref, count_ref, o_ref,
    k_buf, v_buf, msg, stat, r_msg, r_stat,
    k_sem, v_sem, ms_sem, mr_sem, ss_sem, sr_sem, gs_sem, gr_sem,
):
    pairs, group, width = q_ref.shape
    tokens = k_hbm.shape[1]
    blocks = tokens // BLOCK
    own = pairs // n
    heads = count_ref.shape[0]
    slots = chosen_ref.shape[1]
    tiles = msg.shape[1] - own
    scale = 1.0 / math.sqrt(width)
    me = lax.axis_index("seq")

    def owner(k):
        return lax.rem(me + 1 + k, n)

    def source(k):
        return lax.rem(me + 2 * n - 1 - k, n)

    def load(k, hbm, buf, sem):
        return pltpu.make_async_copy(hbm.at[pl.ds(owner(k) * own, own)], buf.at[k], sem.at[k])

    for k in range(n):
        load(k, k_hbm, k_buf, k_sem).start()
        load(k, v_hbm, v_buf, v_sem).start()

    barrier = pltpu.get_barrier_semaphore()
    for k in range(n - 1):
        pl.semaphore_signal(barrier, inc=1, device_id={"seq": owner(k)}, device_id_type=MESH)

    lane = lax.broadcasted_iota(jnp.int32, (ROWS, LANES), 1)
    row = lax.broadcasted_iota(jnp.int32, (ROWS, LANES), 0)

    gate_lane = lax.broadcasted_iota(jnp.int32, (ROWS, gate_ref.shape[2]), 1)
    gate_row = lax.broadcasted_iota(jnp.int32, (ROWS, gate_ref.shape[2]), 0)
    gates = []
    for branch in range(2):
        packed = jnp.zeros((ROWS, LANES), jnp.float32)
        for i in range(own):
            p = me * own + i
            b, h = lax.div(p, heads), lax.rem(p, heads)
            logits = jnp.broadcast_to(gate_ref[branch, pl.ds(b, 1), :], gate_lane.shape)
            column = jnp.sum(
                jnp.where(gate_lane == gate_row + h * group, logits, 0.0), axis=1, keepdims=True
            )
            packed = jnp.where(lane == i, column, packed)
        gates.append(jax.nn.sigmoid(packed))

    pl.semaphore_wait(barrier, n - 1)

    def send_msg(k):
        return pltpu.make_async_remote_copy(
            src_ref=msg.at[k], dst_ref=r_msg.at[k], send_sem=ms_sem.at[k], recv_sem=mr_sem.at[k],
            device_id={"seq": owner(k)}, device_id_type=MESH,
        )

    def send_stat(k):
        return pltpu.make_async_remote_copy(
            src_ref=stat.at[k], dst_ref=r_stat.at[k], send_sem=ss_sem.at[k], recv_sem=sr_sem.at[k],
            device_id={"seq": owner(k)}, device_id_type=MESH,
        )

    def part(k, carry):
        target = owner(k)
        load(k, k_hbm, k_buf, k_sem).wait()
        load(k, v_hbm, v_buf, v_sem).wait()
        stats = jnp.zeros((ROWS, LANES), jnp.float32)
        pooled = [jnp.zeros((ROWS, width), jnp.float32)] * tiles
        for i in range(own):
            p = target * own + i
            b, h = lax.div(p, heads), lax.rem(p, heads)
            length = len_ref[b]
            count = count_ref[h, b]
            chosen = [chosen_ref[h, slot, b] for slot in range(slots)]
            scores = lax.dot_general(
                q_ref[p], k_buf[k, i], (((1,), (1,)), ((), ())), preferred_element_type=jnp.float32
            ) * scale
            tile, base = divmod(i * blocks, ROWS)
            masked, chosen_mask, live_rows = [], [], []
            root_rows = jnp.ones((ROWS, LANES), jnp.float32)
            for j in range(blocks):
                block = me * blocks + j
                filled = jnp.clip(length - block * BLOCK, 0, BLOCK)
                limit = jnp.int32(0)
                for slot in range(slots):
                    hit = jnp.logical_and(chosen[slot] == block, slot < count)
                    limit = jnp.where(hit, filled, limit)
                part_scores = scores[:, j * BLOCK : (j + 1) * BLOCK]
                live = lane < filled
                inside = lane < limit
                filled_rows = jnp.full((ROWS, LANES), filled, jnp.int32)
                root = lax.rsqrt(jnp.maximum(filled_rows, 1).astype(jnp.float32))
                total = jnp.sum(jnp.where(live, part_scores, 0.0), axis=1, keepdims=True)
                pooled_score = jnp.where(filled_rows > 0, total * root, NEG)
                stats = jnp.where(lane == (1 + j) * own + i, pooled_score, stats)
                root_rows = jnp.where(row == base + j, root, root_rows)
                live_rows.append(jnp.where(jnp.logical_and(live, row == base + j), 1.0, 0.0))
                chosen_mask.append(inside)
                masked.append(jnp.where(inside, part_scores, NEG))
            top = functools.reduce(jnp.maximum, masked)
            top = jnp.max(top, axis=1, keepdims=True)
            weights = [
                jnp.where(inside, jnp.exp(m - top), 0.0) for inside, m in zip(chosen_mask, masked)
            ]
            weight_sum = jnp.sum(functools.reduce(jnp.add, weights), axis=1, keepdims=True)
            safe_sum = jnp.maximum(weight_sum, 1.0)
            log_sum = jnp.where(weight_sum > 0.0, top + jnp.log(safe_sum), NEG)
            stats = jnp.where(lane == i, log_sum, stats)
            left = jnp.concatenate(
                [jnp.concatenate(weights, axis=1), jnp.concatenate(live_rows, axis=1)], axis=0
            ).astype(jnp.bfloat16)
            summed = jnp.dot(left, v_buf[k, i], preferred_element_type=jnp.float32)
            msg[k, i] = (summed[:ROWS] / safe_sum).astype(jnp.bfloat16)
            pooled[tile] = pooled[tile] + summed[ROWS:] * root_rows
        for tile in range(tiles):
            msg[k, own + tile] = pooled[tile].astype(jnp.bfloat16)
        stat[k] = stats

        @pl.when(k < n - 1)
        def _():
            send_stat(k).start()
            send_msg(k).start()

        return carry

    lax.fori_loop(0, n, part, 0)

    for k in range(n - 1):
        send_stat(k).wait_recv()
    all_stats = [r_stat[k] for k in range(n - 1)] + [stat[n - 1]]
    top = functools.reduce(jnp.maximum, all_stats)
    shares = [jnp.exp(s - top) for s in all_stats]
    factor = gates[1] / functools.reduce(jnp.add, shares)
    shares = [s * factor for s in shares]
    block_scores = [
        [pltpu.roll(s, LANES - (1 + j) * own, 1) for j in range(blocks)] for s in all_stats
    ]
    flat = [s for per_device in block_scores for s in per_device]
    top = functools.reduce(jnp.maximum, flat)
    block_shares = [[jnp.exp(s - top) for s in per_device] for per_device in block_scores]
    flat = [s for per_device in block_shares for s in per_device]
    factor = gates[0] / functools.reduce(jnp.add, flat)
    block_shares = [[s * factor for s in per_device] for per_device in block_shares]

    for k in range(n - 1):
        send_msg(k).wait_recv()
    for tile in range(tiles):
        tile_rows = [r_msg[k, own + tile].astype(jnp.float32) for k in range(n - 1)]
        tile_rows.append(msg[n - 1, own + tile].astype(jnp.float32))
        for i in range(own):
            if (i * blocks) // ROWS != tile:
                continue
            base = (i * blocks) % ROWS
            total = jnp.zeros((ROWS, width), jnp.float32)
            for k in range(n):
                partial = msg[k, i] if k == n - 1 else r_msg[k, i]
                total += shares[k][:, i : i + 1] * partial.astype(jnp.float32)
                for j in range(blocks):
                    total += (
                        block_shares[k][j][:, i : i + 1] * tile_rows[k][base + j : base + j + 1, :]
                    )
            o_ref[me * own + i] = total.astype(jnp.bfloat16)

    def share(k, holder):
        rows = o_ref.at[pl.ds(holder * own, own)]
        return pltpu.make_async_remote_copy(
            src_ref=rows, dst_ref=rows, send_sem=gs_sem.at[k], recv_sem=gr_sem.at[k],
            device_id={"seq": owner(k)}, device_id_type=MESH,
        )

    for k in range(n - 1):
        share(k, me).start()
    for k in range(n - 1):
        send_stat(k).wait_send()
        send_msg(k).wait_send()
    for k in range(n - 1):
        share(k, source(k)).wait_recv()
    for k in range(n - 1):
        share(k, me).wait_send()


def on_device(n, queries, key_cache, value_cache, gate_logits, lengths, chosen, counts):
    batch_rows, head_count, context, width = key_cache.shape
    pairs = batch_rows * head_count
    group = queries.shape[1] // head_count
    blocks = context // BLOCK
    own = pairs // n
    tiles = -(-own * blocks // ROWS)
    assert pairs % n == 0 and group == ROWS and ROWS % blocks == 0
    assert own * (1 + blocks) <= LANES
    vmem = pl.BlockSpec(memory_space=pltpu.VMEM)
    smem = pl.BlockSpec(memory_space=pltpu.SMEM)
    hbm = pl.BlockSpec(memory_space=pl.ANY)
    dma = pltpu.SemaphoreType.DMA((n,))
    output = pl.pallas_call(
        functools.partial(kernel, n),
        out_shape=jax.ShapeDtypeStruct((pairs, group, width), jnp.bfloat16),
        in_specs=[vmem, hbm, hbm, vmem, smem, smem, smem],
        out_specs=vmem,
        scratch_shapes=[
            pltpu.VMEM((n, own, context, width), jnp.bfloat16),
            pltpu.VMEM((n, own, context, width), jnp.bfloat16),
            pltpu.VMEM((n, own + tiles, group, width), jnp.bfloat16),
            pltpu.VMEM((n, ROWS, LANES), jnp.float32),
            pltpu.VMEM((n, own + tiles, group, width), jnp.bfloat16),
            pltpu.VMEM((n, ROWS, LANES), jnp.float32),
        ] + [dma] * 8,
        compiler_params=pltpu.CompilerParams(collective_id=0, has_side_effects=True),
    )(
        queries.reshape(pairs, group, width),
        key_cache.reshape(pairs, context, width),
        value_cache.reshape(pairs, context, width),
        gate_logits,
        lengths,
        chosen.transpose(1, 2, 0),
        counts.transpose(1, 0),
    )
    return output.reshape(batch_rows, head_count * group, width)


def solution(mesh):
    return jax.shard_map(
        functools.partial(on_device, mesh.shape["seq"]),
        mesh=mesh,
        in_specs=(
            P(("grp", "batch"), "head", None),
            P(("grp", "batch"), "head", "seq", None),
            P(("grp", "batch"), "head", "seq", None),
            P(None, ("grp", "batch"), "head"),
            P(("grp", "batch")),
            P(("grp", "batch"), "head", None),
            P(("grp", "batch"), "head"),
        ),
        out_specs=P(("grp", "batch"), "head", None),
        check_vma=False,
    )
```

time: 87.6 us -> 28.4 us (0.32)
  blocking collectives: 67.3 us -> 0 us
  Pallas kernels: 0 us -> 26.6 us
  matrix products: 14.3 us -> 0 us
  local copies, waits for them, and re-layouts: 3.58 us -> 1.57 us
  other arithmetic: 1.83 us -> 0 us
    all_gather x5 -> x0, blocking collectives: 67.3 us -> none  [the longest x3 38.9 us: combined_all(): lax.all_gather(a.astype(kind), axis)]
    pallas_call x0 -> x1, Pallas kernels: none -> 26.6 us  [on_device(): pl.pallas_call(functools.partial(kernel, n), out_shape=jax.ShapeDtypeStru...]
    dot_general x6 -> x0, matrix products: 14.3 us -> none  [the longest x2 3.93 us: softmax_terms(): jnp.einsum('pgn,pnd->pgd', weights.astype(jnp.bfloat16), value_rows, pref...]
    add x9 -> x0, other arithmetic: 0.89 us -> none  [the longest x3 0.81 us: combine(): first[index + 2] * factor_first[:, :, None]]
where the time goes in v1:
time: 28.4 us; the launch traced here: 28.2 us
  Pallas kernels  26.6 us (94%)
  local copies, waits for them, and re-layouts  1.57 us (6%)
    pallas_call x1, Pallas kernels, on_device(): pl.pallas_call(functools.partial(kernel, n), out_shape=jax.ShapeDtypeStru...  26.6 us
    unnamed x1, local copies, waits for them, and re-layouts  1.57 us

profile of v1, /device:TPU:0, one launch (start us, length us, event | category | flops | bytes accessed | tf_op | source)
XLA Modules:
  0.0 28.2 jit_solution(14949311112217429985)
XLA Ops:
  0.0 26.6 %shard_map.73 = bf16[64,8,128]{2,1,0:T(8,128)(2,1)} custom-call(bf16[64,8,128]{2,1,0:T(8,128)(2,1)} %bitcast.9, bf16[64,256,128]{2,1,0:T(8,128)(2,1)} %bitcast.6, bf16[64,256,128]{2,1,0:T(8,128)(2,1)} %bitcast.7, f32[2,16,32]{2,1,0:T(8,128)} %gate_ref.1, s32[16]{0:T(128)} %len_ref.1, s32[4,2,16]{2,1,0:T(2,128)} %bitcast.10, s32[4,16]{1,0:T(4,128)} %bitcast.11), custom_call_target="tpu_custom_call" | custom-call | tf_op jit(solution)/shard_map/pallas_call | solution.py:214
  26.6 1.6 %copy.9 = bf16[16,32,128]{2,1,0:T(8,128)(2,1)} copy(bf16[16,32,128]{2,1,0:T(8,128)(2,1)} %bitcast.8) | data formatting | bytes 262144

commit v2 on v1

v2 whole, which is shorter than its diff:
```python
import functools
import math

import jax
import jax.numpy as jnp
from jax import lax
from jax.experimental import pallas as pl
from jax.experimental.pallas import tpu as pltpu
from jax.sharding import PartitionSpec as P

BLOCK = 128
LANES = 128
ROWS = 8
NEG = -1e30
MESH = pl.DeviceIdType.MESH


def kernel(
    n, q_ref, k_hbm, v_hbm, gate_ref, len_ref, chosen_ref, count_ref, o_ref,
    k_buf, v_buf, msg, stat, r_msg, r_stat,
    k_sem, v_sem, ms_sem, mr_sem, ss_sem, sr_sem, gs_sem, gr_sem,
):
    pairs, group, width = q_ref.shape
    tokens = k_hbm.shape[1]
    blocks = tokens // BLOCK
    own = pairs // n
    heads = count_ref.shape[0]
    slots = chosen_ref.shape[1]
    tiles = msg.shape[1] - own
    scale = 1.0 / math.sqrt(width)
    me = lax.axis_index("seq")

    def owner(k):
        return lax.rem(me + 1 + k, n)

    def source(k):
        return lax.rem(me + 2 * n - 1 - k, n)

    def load(k, hbm, buf, sem):
        return pltpu.make_async_copy(hbm.at[pl.ds(owner(k) * own, own)], buf.at[k], sem.at[k])

    for k in range(n):
        load(k, k_hbm, k_buf, k_sem).start()
        load(k, v_hbm, v_buf, v_sem).start()

    barrier = pltpu.get_barrier_semaphore()
    for k in range(n - 1):
        pl.semaphore_signal(barrier, inc=1, device_id={"seq": owner(k)}, device_id_type=MESH)

    lane = lax.broadcasted_iota(jnp.int32, (ROWS, LANES), 1)
    row = lax.broadcasted_iota(jnp.int32, (ROWS, LANES), 0)

    lane_pair = lax.div(lane, group)

    def gate_row(branch):
        if own % heads == 0:
            first = me * (own // heads)
            pieces = [gate_ref[branch, pl.ds(first + r, 1), :] for r in range(own // heads)]
        else:
            first = me * own
            line = gate_ref[branch, pl.ds(lax.div(first, heads), 1), :]
            picked = line[:, : own * group]
            for o in range(1, heads // own):
                here = lax.rem(first, heads) == o * own
                picked = jnp.where(here, line[:, o * own * group : (o + 1) * own * group], picked)
            pieces = [picked]
        if own * group < LANES:
            pieces.append(jnp.zeros((1, LANES - own * group), jnp.float32))
        return jax.nn.sigmoid(jnp.concatenate(pieces, axis=1))

    gates = jnp.where(row == 0, gate_row(1), gate_row(0))
    token = lax.broadcasted_iota(jnp.int32, (BLOCK, LANES), 0)

    pl.semaphore_wait(barrier, n - 1)

    def send_msg(k):
        return pltpu.make_async_remote_copy(
            src_ref=msg.at[k], dst_ref=r_msg.at[k], send_sem=ms_sem.at[k], recv_sem=mr_sem.at[k],
            device_id={"seq": owner(k)}, device_id_type=MESH,
        )

    def send_stat(k):
        return pltpu.make_async_remote_copy(
            src_ref=stat.at[k], dst_ref=r_stat.at[k], send_sem=ss_sem.at[k], recv_sem=sr_sem.at[k],
            device_id={"seq": owner(k)}, device_id_type=MESH,
        )

    def part(k, carry):
        target = owner(k)
        first = target * own
        lengths = [len_ref[lax.div(first + i, heads)] for i in range(own)]

        def spread(values):
            line = jnp.full((1, LANES), values[0], jnp.int32)
            for i in range(1, own):
                line = jnp.where(lane_pair[:1] == i, values[i], line)
            return line

        length_line = spread(lengths)
        pair_ids = [(lax.rem(first + i, heads), lax.div(first + i, heads)) for i in range(own)]
        count_line = spread([count_ref[h, b] for h, b in pair_ids])
        chosen_lines = [spread([chosen_ref[h, slot, b] for h, b in pair_ids]) for slot in range(slots)]
        chosen_lines = [jnp.where(slot < count_line, line, -1) for slot, line in enumerate(chosen_lines)]

        rows = q_ref[pl.ds(first, own)].astype(jnp.float32).reshape(own * group, width)
        if own * group < LANES:
            rows = jnp.concatenate([rows, jnp.zeros((LANES - own * group, width), jnp.float32)], axis=0)
        columns = rows.T
        load(k, k_hbm, k_buf, k_sem).wait()
        scores = None
        for i in range(0, own, 2):
            both = range(i, min(i + 2, own))
            held = jnp.concatenate(
                [jnp.where(lane_pair[:1] == p, columns, 0.0) for p in both], axis=0
            ).astype(jnp.bfloat16)
            keys = jnp.concatenate([k_buf[k, p] for p in both], axis=1)
            product = jnp.dot(keys, held, preferred_element_type=jnp.float32)
            scores = product if scores is None else scores + product
        scores = scores * scale

        stats = jnp.zeros((ROWS, LANES), jnp.float32)
        masked, inside = [], []
        for j in range(blocks):
            block = me * blocks + j
            filled = jnp.clip(length_line - block * BLOCK, 0, BLOCK)
            hits = [line == block for line in chosen_lines]
            limit = jnp.where(functools.reduce(jnp.logical_or, hits), filled, 0)
            block_scores = scores[j * BLOCK : (j + 1) * BLOCK]
            root = lax.rsqrt(jnp.maximum(filled, 1).astype(jnp.float32))
            total = jnp.sum(jnp.where(token < filled, block_scores, 0.0), axis=0, keepdims=True)
            stats = jnp.where(row == 1 + j, jnp.where(filled > 0, total * root, NEG), stats)
            inside.append(token < limit)
            masked.append(jnp.where(inside[j], block_scores, NEG))
        top = jnp.max(functools.reduce(jnp.maximum, masked), axis=0, keepdims=True)
        weights = [jnp.where(i, jnp.exp(m - top), 0.0) for i, m in zip(inside, masked)]
        weight_sum = jnp.sum(functools.reduce(jnp.add, weights), axis=0, keepdims=True)
        safe_sum = jnp.maximum(weight_sum, 1.0)
        log_sum = jnp.where(weight_sum > 0.0, top + jnp.log(safe_sum), NEG)
        stats = jnp.where(row == 0, log_sum, stats)
        stat[k] = stats
        inverse = 1.0 / safe_sum
        weight_rows = jnp.concatenate([(w * inverse).T for w in weights], axis=1)

        load(k, v_hbm, v_buf, v_sem).wait()
        per_tile = ROWS // blocks
        for tile in range(tiles):
            members = range(tile * per_tile, min((tile + 1) * per_tile, own))
            length_rows = jnp.zeros((ROWS, LANES), jnp.int32)
            for at, i in enumerate(members):
                length_rows = jnp.where(lax.div(row, blocks) == at, lengths[i], length_rows)
            start_rows = (me * blocks + lax.rem(row, blocks)) * BLOCK
            filled_rows = jnp.clip(length_rows - start_rows, 0, BLOCK)
            root_rows = lax.rsqrt(jnp.maximum(filled_rows, 1).astype(jnp.float32))
            live = lane < filled_rows
            pooled = jnp.zeros((ROWS, width), jnp.float32)
            for at, i in enumerate(members):
                live_rows = jnp.concatenate(
                    [jnp.where(live & (row == at * blocks + j), 1.0, 0.0) for j in range(blocks)], axis=1
                )
                left = jnp.concatenate([weight_rows[i * group : (i + 1) * group], live_rows], axis=0)
                summed = jnp.dot(
                    left.astype(jnp.bfloat16), v_buf[k, i], preferred_element_type=jnp.float32
                )
                msg[k, i] = summed[:group].astype(jnp.bfloat16)
                pooled = pooled + summed[group:]
            msg[k, own + tile] = (pooled * root_rows).astype(jnp.bfloat16)

        @pl.when(k < n - 1)
        def _():
            send_stat(k).start()
            send_msg(k).start()

        return carry

    lax.fori_loop(0, n, part, 0)

    for k in range(n - 1):
        send_stat(k).wait_recv()
    all_stats = [r_stat[k] for k in range(n - 1)] + [stat[n - 1]]
    top = functools.reduce(jnp.maximum, all_stats)
    block_row = (row >= 1) & (row <= blocks)
    block_top = jnp.max(jnp.where(block_row, top, NEG), axis=0, keepdims=True)
    top = jnp.where(row == 0, top, block_top)
    shares = [jnp.where(row <= blocks, jnp.exp(s - top), 0.0) for s in all_stats]
    total = functools.reduce(jnp.add, shares)
    block_total = jnp.sum(jnp.where(block_row, total, 0.0), axis=0, keepdims=True)
    factor = gates / jnp.where(row == 0, total, block_total)
    shares = [s * factor for s in shares]
    per_turn = LANES // ROWS
    turned = []
    for k in range(0, n, per_turn):
        stack = shares[k : k + per_turn]
        if len(stack) < per_turn:
            stack.append(jnp.zeros((LANES - len(stack) * ROWS, LANES), jnp.float32))
        turned.append(jnp.concatenate(stack, axis=0).T)

    def coefficient(k, i, which):
        at = (k % per_turn) * ROWS + which
        return turned[k // per_turn][i * group : (i + 1) * group, at : at + 1]

    for k in range(n - 1):
        send_msg(k).wait_recv()
    for tile in range(tiles):
        tile_rows = [r_msg[k, own + tile].astype(jnp.float32) for k in range(n - 1)]
        tile_rows.append(msg[n - 1, own + tile].astype(jnp.float32))
        for i in range(own):
            if (i * blocks) // ROWS != tile:
                continue
            base = (i * blocks) % ROWS
            total = jnp.zeros((ROWS, width), jnp.float32)
            for k in range(n):
                partial = msg[k, i] if k == n - 1 else r_msg[k, i]
                total += coefficient(k, i, 0) * partial.astype(jnp.float32)
                for j in range(blocks):
                    total += coefficient(k, i, 1 + j) * tile_rows[k][base + j : base + j + 1, :]
            o_ref[me * own + i] = total.astype(jnp.bfloat16)

    def share(k, holder):
        rows = o_ref.at[pl.ds(holder * own, own)]
        return pltpu.make_async_remote_copy(
            src_ref=rows, dst_ref=rows, send_sem=gs_sem.at[k], recv_sem=gr_sem.at[k],
            device_id={"seq": owner(k)}, device_id_type=MESH,
        )

    for k in range(n - 1):
        share(k, me).start()
    for k in range(n - 1):
        send_stat(k).wait_send()
        send_msg(k).wait_send()
    for k in range(n - 1):
        share(k, source(k)).wait_recv()
    for k in range(n - 1):
        share(k, me).wait_send()


def on_device(n, queries, key_cache, value_cache, gate_logits, lengths, chosen, counts):
    batch_rows, head_count, context, width = key_cache.shape
    pairs = batch_rows * head_count
    group = queries.shape[1] // head_count
    blocks = context // BLOCK
    own = pairs // n
    tiles = -(-own * blocks // ROWS)
    assert pairs % n == 0 and group == ROWS and ROWS % blocks == 0
    assert own * group <= LANES and 1 + blocks <= ROWS and width == LANES
    vmem = pl.BlockSpec(memory_space=pltpu.VMEM)
    smem = pl.BlockSpec(memory_space=pltpu.SMEM)
    hbm = pl.BlockSpec(memory_space=pl.ANY)
    dma = pltpu.SemaphoreType.DMA((n,))
    output = pl.pallas_call(
        functools.partial(kernel, n),
        out_shape=jax.ShapeDtypeStruct((pairs, group, width), jnp.bfloat16),
        in_specs=[vmem, hbm, hbm, vmem, smem, smem, smem],
        out_specs=vmem,
        scratch_shapes=[
            pltpu.VMEM((n, own, context, width), jnp.bfloat16),
            pltpu.VMEM((n, own, context, width), jnp.bfloat16),
            pltpu.VMEM((n, own + tiles, group, width), jnp.bfloat16),
            pltpu.VMEM((n, ROWS, LANES), jnp.float32),
            pltpu.VMEM((n, own + tiles, group, width), jnp.bfloat16),
            pltpu.VMEM((n, ROWS, LANES), jnp.float32),
        ] + [dma] * 8,
        compiler_params=pltpu.CompilerParams(collective_id=0, has_side_effects=True),
    )(
        queries.reshape(pairs, group, width),
        key_cache.reshape(pairs, context, width),
        value_cache.reshape(pairs, context, width),
        gate_logits,
        lengths,
        chosen.transpose(1, 2, 0),
        counts.transpose(1, 0),
    )
    return output.reshape(batch_rows, head_count * group, width)


def solution(mesh):
    return jax.shard_map(
        functools.partial(on_device, mesh.shape["seq"]),
        mesh=mesh,
        in_specs=(
            P(("grp", "batch"), "head", None),
            P(("grp", "batch"), "head", "seq", None),
            P(("grp", "batch"), "head", "seq", None),
            P(None, ("grp", "batch"), "head"),
            P(("grp", "batch")),
            P(("grp", "batch"), "head", None),
            P(("grp", "batch"), "head"),
        ),
        out_specs=P(("grp", "batch"), "head", None),
        check_vma=False,
    )
```

time: 28.4 us -> 20.1 us (0.71)
  Pallas kernels: 26.6 us -> 18.4 us
    pallas_call x1, Pallas kernels: 26.6 us -> 18.4 us  [on_device(): pl.pallas_call(functools.partial(kernel, n), out_shape=jax.ShapeDtypeStru...]
where the time goes in v2:
time: 20.1 us; the launch traced here: 20 us
  Pallas kernels  18.4 us (92%)
  local copies, waits for them, and re-layouts  1.57 us (8%)
    pallas_call x1, Pallas kernels, on_device(): pl.pallas_call(functools.partial(kernel, n), out_shape=jax.ShapeDtypeStru...  18.4 us
    unnamed x1, local copies, waits for them, and re-layouts  1.57 us

profile of v2, /device:TPU:0, one launch (start us, length us, event | category | flops | bytes accessed | tf_op | source)
XLA Modules:
  0.0 20.0 jit_solution(5998261084639764686)
XLA Ops:
  0.0 18.4 %shard_map.73 = bf16[64,8,128]{2,1,0:T(8,128)(2,1)} custom-call(bf16[64,8,128]{2,1,0:T(8,128)(2,1)} %bitcast.9, bf16[64,256,128]{2,1,0:T(8,128)(2,1)} %bitcast.6, bf16[64,256,128]{2,1,0:T(8,128)(2,1)} %bitcast.7, f32[2,16,32]{2,1,0:T(8,128)} %gate_ref.1, s32[16]{0:T(128)} %len_ref.1, s32[4,2,16]{2,1,0:T(2,128)} %bitcast.10, s32[4,16]{1,0:T(4,128)} %bitcast.11), custom_call_target="tpu_custom_call" | custom-call | tf_op jit(solution)/shard_map/pallas_call | solution.py:249
  18.4 1.6 %copy.9 = bf16[16,32,128]{2,1,0:T(8,128)(2,1)} copy(bf16[16,32,128]{2,1,0:T(8,128)(2,1)} %bitcast.8) | data formatting | bytes 262144

commit v3 on v2

--- a/solution.py
+++ b/solution.py
@@ -70,8 +70,6 @@
 
     gates = jnp.where(row == 0, gate_row(1), gate_row(0))
     token = lax.broadcasted_iota(jnp.int32, (BLOCK, LANES), 0)
-
-    pl.semaphore_wait(barrier, n - 1)
 
     def send_msg(k):
         return pltpu.make_async_remote_copy(
@@ -165,6 +163,10 @@
                 pooled = pooled + summed[group:]
             msg[k, own + tile] = (pooled * root_rows).astype(jnp.bfloat16)
 
+        @pl.when(k == 0)
+        def _():
+            pl.semaphore_wait(barrier, n - 1)
+
         @pl.when(k < n - 1)
         def _():
             send_stat(k).start()
@@ -248,7 +250,7 @@
     dma = pltpu.SemaphoreType.DMA((n,))
     output = pl.pallas_call(
         functools.partial(kernel, n),
-        out_shape=jax.ShapeDtypeStruct((pairs, group, width), jnp.bfloat16),
+        out_shape=pltpu.VMEM((pairs, group, width), jnp.bfloat16),
         in_specs=[vmem, hbm, hbm, vmem, smem, smem, smem],
         out_specs=vmem,
         scratch_shapes=[

time: 20.1 us -> 17.5 us (0.87)
  Pallas kernels: 18.4 us -> 16.7 us
  local copies, waits for them, and re-layouts: 1.57 us -> 0.66 us
    pallas_call x1, Pallas kernels: 18.4 us -> 16.7 us  [on_device(): pl.pallas_call(functools.partial(kernel, n), out_shape=pltpu.VMEM((pairs,...]
    unnamed x1, local copies, waits for them, and re-layouts: 1.57 us -> 0.66 us
where the time goes in v3:
time: 17.5 us; the launch traced here: 17.3 us
  Pallas kernels  16.7 us (95%)
  local copies, waits for them, and re-layouts  0.66 us (4%)
    pallas_call x1, Pallas kernels, on_device(): pl.pallas_call(functools.partial(kernel, n), out_shape=pltpu.VMEM((pairs,...  16.7 us
    unnamed x1, local copies, waits for them, and re-layouts  0.66 us

profile of v3, /device:TPU:0, one launch (start us, length us, event | category | flops | bytes accessed | tf_op | source)
XLA Modules:
  0.0 17.3 jit_solution(3262020315173779026)
XLA Ops:
  0.0 16.7 %shard_map.73 = bf16[64,8,128]{2,1,0:T(8,128)(2,1)S(1)} custom-call(bf16[64,8,128]{2,1,0:T(8,128)(2,1)} %bitcast.9, bf16[64,256,128]{2,1,0:T(8,128)(2,1)} %bitcast.7, bf16[64,256,128]{2,1,0:T(8,128)(2,1)} %bitcast.8, f32[2,16,32]{2,1,0:T(8,128)} %gate_ref.1, s32[16]{0:T(128)} %len_ref.1, s32[4,2,16]{2,1,0:T(2,128)} %bitcast.10, s32[4,16]{1,0:T(4,128)} %bitcast.11), custom_call_target="tpu_custom_call" | custom-call | tf_op jit(solution)/shard_map/pallas_call | solution.py:251
  16.7 0.7 %copy.9 = bf16[16,32,128]{2,1,0:T(8,128)(2,1)} copy(bf16[16,32,128]{2,1,0:T(8,128)(2,1)S(1)} %bitcast.6) | data formatting | bytes 262144

commit v4 on v3

--- a/solution.py
+++ b/solution.py
@@ -30,34 +30,43 @@
     scale = 1.0 / math.sqrt(width)
     me = lax.axis_index("seq")
 
-    def owner(k):
-        return lax.rem(me + 1 + k, n)
-
-    def source(k):
-        return lax.rem(me + 2 * n - 1 - k, n)
+    holders = n // 2
+    turns = n // holders
+    low = (n - holders) // 2
+
+    far = jnp.where(me < n // 2, (holders + 1) // 2, 0)
+
+    def chunk_at(k):
+        return lax.rem(lax.rem(k, holders) + far, holders) * turns + lax.div(k, holders)
+
+    def owner(c):
+        return low + lax.div(c, turns)
+
+    def peer(r):
+        return lax.rem(me + r, n)
 
     def load(k, hbm, buf, sem):
-        return pltpu.make_async_copy(hbm.at[pl.ds(owner(k) * own, own)], buf.at[k], sem.at[k])
+        return pltpu.make_async_copy(hbm.at[pl.ds(chunk_at(k) * own, own)], buf.at[k], sem.at[k])
 
     for k in range(n):
         load(k, k_hbm, k_buf, k_sem).start()
         load(k, v_hbm, v_buf, v_sem).start()
 
     barrier = pltpu.get_barrier_semaphore()
-    for k in range(n - 1):
-        pl.semaphore_signal(barrier, inc=1, device_id={"seq": owner(k)}, device_id_type=MESH)
+    for r in range(1, n):
+        pl.semaphore_signal(barrier, inc=1, device_id={"seq": peer(r)}, device_id_type=MESH)
 
     lane = lax.broadcasted_iota(jnp.int32, (ROWS, LANES), 1)
     row = lax.broadcasted_iota(jnp.int32, (ROWS, LANES), 0)
 
     lane_pair = lax.div(lane, group)
 
-    def gate_row(branch):
+    def gate_row(branch, first_pair):
         if own % heads == 0:
-            first = me * (own // heads)
+            first = lax.div(first_pair, heads)
             pieces = [gate_ref[branch, pl.ds(first + r, 1), :] for r in range(own // heads)]
         else:
-            first = me * own
+            first = first_pair
             line = gate_ref[branch, pl.ds(lax.div(first, heads), 1), :]
             picked = line[:, : own * group]
             for o in range(1, heads // own):
@@ -68,23 +77,30 @@
             pieces.append(jnp.zeros((1, LANES - own * group), jnp.float32))
         return jax.nn.sigmoid(jnp.concatenate(pieces, axis=1))
 
-    gates = jnp.where(row == 0, gate_row(1), gate_row(0))
     token = lax.broadcasted_iota(jnp.int32, (BLOCK, LANES), 0)
 
-    def send_msg(k):
+    def send(k, held, landed, send_sem, recv_sem):
+        c = chunk_at(k)
+        turn = lax.rem(c, turns)
+        slot = lax.rem(me - owner(c) + n, n) - 1
         return pltpu.make_async_remote_copy(
-            src_ref=msg.at[k], dst_ref=r_msg.at[k], send_sem=ms_sem.at[k], recv_sem=mr_sem.at[k],
-            device_id={"seq": owner(k)}, device_id_type=MESH,
+            src_ref=held.at[k], dst_ref=landed.at[turn, slot],
+            send_sem=send_sem.at[k], recv_sem=recv_sem.at[turn, slot],
+            device_id={"seq": owner(c)}, device_id_type=MESH,
         )
 
-    def send_stat(k):
+    def arrival(turn, slot, held, landed, send_sem, recv_sem):
         return pltpu.make_async_remote_copy(
-            src_ref=stat.at[k], dst_ref=r_stat.at[k], send_sem=ss_sem.at[k], recv_sem=sr_sem.at[k],
-            device_id={"seq": owner(k)}, device_id_type=MESH,
+            src_ref=held.at[0], dst_ref=landed.at[turn, slot],
+            send_sem=send_sem.at[0], recv_sem=recv_sem.at[turn, slot],
+            device_id={"seq": peer(1 + slot)}, device_id_type=MESH,
         )
 
+    stat_path = (stat, r_stat, ss_sem, sr_sem)
+    msg_path = (msg, r_msg, ms_sem, mr_sem)
+
     def part(k, carry):
-        target = owner(k)
+        target = chunk_at(k)
         first = target * own
         lengths = [len_ref[lax.div(first + i, heads)] for i in range(own)]
 
@@ -167,72 +183,104 @@
         def _():
             pl.semaphore_wait(barrier, n - 1)
 
-        @pl.when(k < n - 1)
+        @pl.when(owner(target) != me)
         def _():
-            send_stat(k).start()
-            send_msg(k).start()
+            send(k, *stat_path).start()
+            send(k, *msg_path).start()
 
         return carry
 
     lax.fori_loop(0, n, part, 0)
 
-    for k in range(n - 1):
-        send_stat(k).wait_recv()
-    all_stats = [r_stat[k] for k in range(n - 1)] + [stat[n - 1]]
-    top = functools.reduce(jnp.maximum, all_stats)
-    block_row = (row >= 1) & (row <= blocks)
-    block_top = jnp.max(jnp.where(block_row, top, NEG), axis=0, keepdims=True)
-    top = jnp.where(row == 0, top, block_top)
-    shares = [jnp.where(row <= blocks, jnp.exp(s - top), 0.0) for s in all_stats]
-    total = functools.reduce(jnp.add, shares)
-    block_total = jnp.sum(jnp.where(block_row, total, 0.0), axis=0, keepdims=True)
-    factor = gates / jnp.where(row == 0, total, block_total)
-    shares = [s * factor for s in shares]
-    per_turn = LANES // ROWS
-    turned = []
-    for k in range(0, n, per_turn):
-        stack = shares[k : k + per_turn]
-        if len(stack) < per_turn:
-            stack.append(jnp.zeros((LANES - len(stack) * ROWS, LANES), jnp.float32))
-        turned.append(jnp.concatenate(stack, axis=0).T)
-
-    def coefficient(k, i, which):
-        at = (k % per_turn) * ROWS + which
-        return turned[k // per_turn][i * group : (i + 1) * group, at : at + 1]
-
-    for k in range(n - 1):
-        send_msg(k).wait_recv()
-    for tile in range(tiles):
-        tile_rows = [r_msg[k, own + tile].astype(jnp.float32) for k in range(n - 1)]
-        tile_rows.append(msg[n - 1, own + tile].astype(jnp.float32))
-        for i in range(own):
-            if (i * blocks) // ROWS != tile:
-                continue
-            base = (i * blocks) % ROWS
-            total = jnp.zeros((ROWS, width), jnp.float32)
-            for k in range(n):
-                partial = msg[k, i] if k == n - 1 else r_msg[k, i]
-                total += coefficient(k, i, 0) * partial.astype(jnp.float32)
-                for j in range(blocks):
-                    total += coefficient(k, i, 1 + j) * tile_rows[k][base + j : base + j + 1, :]
-            o_ref[me * own + i] = total.astype(jnp.bfloat16)
-
-    def share(k, holder):
-        rows = o_ref.at[pl.ds(holder * own, own)]
+    def share(turn, r):
+        c = (me - low) * turns + turn
+        rows = o_ref.at[pl.ds(c * own, own)]
         return pltpu.make_async_remote_copy(
-            src_ref=rows, dst_ref=rows, send_sem=gs_sem.at[k], recv_sem=gr_sem.at[k],
-            device_id={"seq": owner(k)}, device_id_type=MESH,
+            src_ref=rows, dst_ref=rows, send_sem=gs_sem.at[turn, r - 1], recv_sem=gr_sem.at[c],
+            device_id={"seq": peer(r)}, device_id_type=MESH,
         )
 
-    for k in range(n - 1):
-        share(k, me).start()
-    for k in range(n - 1):
-        send_stat(k).wait_send()
-        send_msg(k).wait_send()
-    for k in range(n - 1):
-        share(k, source(k)).wait_recv()
-    for k in range(n - 1):
-        share(k, me).wait_send()
+    def finish(turn):
+        c = (me - low) * turns + turn
+        home = turn * holders + lax.rem(me - low + holders - far, holders)
+        gates = jnp.where(row == 0, gate_row(1, c * own), gate_row(0, c * own))
+        for slot in range(n - 1):
+            arrival(turn, slot, *stat_path).wait_recv()
+        all_stats = [r_stat[turn, slot] for slot in range(n - 1)] + [stat[home]]
+        top = functools.reduce(jnp.maximum, all_stats)
+        block_row = (row >= 1) & (row <= blocks)
+        block_top = jnp.max(jnp.where(block_row, top, NEG), axis=0, keepdims=True)
+        top = jnp.where(row == 0, top, block_top)
+        shares = [jnp.where(row <= blocks, jnp.exp(s - top), 0.0) for s in all_stats]
+        total = functools.reduce(jnp.add, shares)
+        block_total = jnp.sum(jnp.where(block_row, total, 0.0), axis=0, keepdims=True)
+        factor = gates / jnp.where(row == 0, total, block_total)
+        shares = [s * factor for s in shares]
+        per_turn = LANES // ROWS
+        turned = []
+        for k in range(0, n, per_turn):
+            stack = shares[k : k + per_turn]
+            if len(stack) < per_turn:
+                stack.append(jnp.zeros((LANES - len(stack) * ROWS, LANES), jnp.float32))
+            turned.append(jnp.concatenate(stack, axis=0).T)
+
+        def coefficient(k, i, which):
+            at = (k % per_turn) * ROWS + which
+            return turned[k // per_turn][i * group : (i + 1) * group, at : at + 1]
+
+        for slot in range(n - 1):
+            arrival(turn, slot, *msg_path).wait_recv()
+        for tile in range(tiles):
+            tile_rows = [r_msg[turn, slot, own + tile].astype(jnp.float32) for slot in range(n - 1)]
+            tile_rows.append(msg[home, own + tile].astype(jnp.float32))
+            for i in range(own):
+                if (i * blocks) // ROWS != tile:
+                    continue
+                base = (i * blocks) % ROWS
+                total = jnp.zeros((ROWS, width), jnp.float32)
+                for k in range(n):
+                    partial = msg[home, i] if k == n - 1 else r_msg[turn, k, i]
+                    total += coefficient(k, i, 0) * partial.astype(jnp.float32)
+                    for j in range(blocks):
+                        total += coefficient(k, i, 1 + j) * tile_rows[k][base + j : base + j + 1, :]
+                o_ref[c * own + i] = total.astype(jnp.bfloat16)
+        for r in range(1, n):
+            share(turn, r).start()
+
+    holds = jnp.logical_and(me >= low, me < low + holders)
+
+    @pl.when(holds)
+    def _():
+        for turn in range(turns):
+            finish(turn)
+
+    def drain(k, carry):
+        @pl.when(owner(chunk_at(k)) != me)
+        def _():
+            send(k, *stat_path).wait_send()
+            send(k, *msg_path).wait_send()
+
+        return carry
+
+    def collect(c, carry):
+        @pl.when(owner(c) != me)
+        def _():
+            rows = o_ref.at[pl.ds(c * own, own)]
+            pltpu.make_async_remote_copy(
+                src_ref=rows, dst_ref=rows, send_sem=gs_sem.at[0, 0], recv_sem=gr_sem.at[c],
+                device_id={"seq": owner(c)}, device_id_type=MESH,
+            ).wait_recv()
+
+        return carry
+
+    lax.fori_loop(0, n, drain, 0)
+    lax.fori_loop(0, n, collect, 0)
+
+    @pl.when(holds)
+    def _():
+        for turn in range(turns):
+            for r in range(1, n):
+                share(turn, r).wait_send()
 
 
 def on_device(n, queries, key_cache, value_cache, gate_logits, lengths, chosen, counts):
@@ -242,12 +290,14 @@
     blocks = context // BLOCK
     own = pairs // n
     tiles = -(-own * blocks // ROWS)
-    assert pairs % n == 0 and group == ROWS and ROWS % blocks == 0
+    assert n % 2 == 0 and pairs % n == 0 and group == ROWS and ROWS % blocks == 0
     assert own * group <= LANES and 1 + blocks <= ROWS and width == LANES
     vmem = pl.BlockSpec(memory_space=pltpu.VMEM)
     smem = pl.BlockSpec(memory_space=pltpu.SMEM)
     hbm = pl.BlockSpec(memory_space=pl.ANY)
+    turns = n // (n // 2)
     dma = pltpu.SemaphoreType.DMA((n,))
+    dma2 = pltpu.SemaphoreType.DMA((turns, n - 1))
     output = pl.pallas_call(
         functools.partial(kernel, n),
         out_shape=pltpu.VMEM((pairs, group, width), jnp.bfloat16),
@@ -258,9 +308,10 @@
             pltpu.VMEM((n, own, context, width), jnp.bfloat16),
             pltpu.VMEM((n, own + tiles, group, width), jnp.bfloat16),
             pltpu.VMEM((n, ROWS, LANES), jnp.float32),
-            pltpu.VMEM((n, own + tiles, group, width), jnp.bfloat16),
-            pltpu.VMEM((n, ROWS, LANES), jnp.float32),
-        ] + [dma] * 8,
+            pltpu.VMEM((turns, n - 1, own + tiles, group, width), jnp.bfloat16),
+            pltpu.VMEM((turns, n - 1, ROWS, LANES), jnp.float32),
+            dma, dma, dma, dma2, dma, dma2, dma2, dma,
+        ],
         compiler_params=pltpu.CompilerParams(collective_id=0, has_side_effects=True),
     )(
         queries.reshape(pairs, group, width),

time: 17.5 us -> 17.5 us (level)
  no operation moved by 1% of the time
where the time goes in v4:
time: 17.5 us; the launch traced here: 17.3 us
  Pallas kernels  16.7 us (95%)
  local copies, waits for them, and re-layouts  0.66 us (4%)
    pallas_call x1, Pallas kernels, on_device(): pl.pallas_call(functools.partial(kernel, n), out_shape=pltpu.VMEM((pairs,...  16.7 us
    unnamed x1, local copies, waits for them, and re-layouts  0.66 us

profile of v4, /device:TPU:0, one launch (start us, length us, event | category | flops | bytes accessed | tf_op | source)
XLA Modules:
  0.0 17.3 jit_solution(4712042784869161853)
XLA Ops:
  0.0 16.7 %shard_map.73 = bf16[64,8,128]{2,1,0:T(8,128)(2,1)S(1)} custom-call(bf16[64,8,128]{2,1,0:T(8,128)(2,1)} %bitcast.9, bf16[64,256,128]{2,1,0:T(8,128)(2,1)} %bitcast.7, bf16[64,256,128]{2,1,0:T(8,128)(2,1)} %bitcast.8, f32[2,16,32]{2,1,0:T(8,128)} %gate_ref.1, s32[16]{0:T(128)} %len_ref.1, s32[4,2,16]{2,1,0:T(2,128)} %bitcast.10, s32[4,16]{1,0:T(4,128)} %bitcast.11), custom_call_target="tpu_custom_call" | custom-call | tf_op jit(solution)/shard_map/pallas_call | solution.py:301
  16.7 0.7 %copy.9 = bf16[16,32,128]{2,1,0:T(8,128)(2,1)} copy(bf16[16,32,128]{2,1,0:T(8,128)(2,1)S(1)} %bitcast.6) | data formatting | bytes 262144

commit v5 on v4

--- a/solution.py
+++ b/solution.py
@@ -53,8 +53,13 @@
         load(k, v_hbm, v_buf, v_sem).start()
 
     barrier = pltpu.get_barrier_semaphore()
+    holds = jnp.logical_and(me >= low, me < low + holders)
     for r in range(1, n):
-        pl.semaphore_signal(barrier, inc=1, device_id={"seq": peer(r)}, device_id_type=MESH)
+        other = peer(r)
+
+        @pl.when(jnp.logical_or(holds, jnp.logical_and(other >= low, other < low + holders)))
+        def _(other=other):
+            pl.semaphore_signal(barrier, inc=1, device_id={"seq": other}, device_id_type=MESH)
 
     lane = lax.broadcasted_iota(jnp.int32, (ROWS, LANES), 1)
     row = lax.broadcasted_iota(jnp.int32, (ROWS, LANES), 0)
@@ -77,6 +82,10 @@
             pieces.append(jnp.zeros((1, LANES - own * group), jnp.float32))
         return jax.nn.sigmoid(jnp.concatenate(pieces, axis=1))
 
+    all_gates = []
+    for turn in range(turns):
+        gate_pair = lax.rem((me - low) * turns + turn + n, n) * own
+        all_gates.append(jnp.where(row == 0, gate_row(1, gate_pair), gate_row(0, gate_pair)))
     token = lax.broadcasted_iota(jnp.int32, (BLOCK, LANES), 0)
 
     def send(k, held, landed, send_sem, recv_sem):
@@ -181,7 +190,7 @@
 
         @pl.when(k == 0)
         def _():
-            pl.semaphore_wait(barrier, n - 1)
+            pl.semaphore_wait(barrier, jnp.where(holds, n - 1, holders))
 
         @pl.when(owner(target) != me)
         def _():
@@ -190,7 +199,7 @@
 
         return carry
 
-    lax.fori_loop(0, n, part, 0)
+    lax.fori_loop(0, n, part, 0, unroll=4)
 
     def share(turn, r):
         c = (me - low) * turns + turn
@@ -203,7 +212,7 @@
     def finish(turn):
         c = (me - low) * turns + turn
         home = turn * holders + lax.rem(me - low + holders - far, holders)
-        gates = jnp.where(row == 0, gate_row(1, c * own), gate_row(0, c * own))
+        gates = all_gates[turn]
         for slot in range(n - 1):
             arrival(turn, slot, *stat_path).wait_recv()
         all_stats = [r_stat[turn, slot] for slot in range(n - 1)] + [stat[home]]
@@ -246,8 +255,6 @@
                 o_ref[c * own + i] = total.astype(jnp.bfloat16)
         for r in range(1, n):
             share(turn, r).start()
-
-    holds = jnp.logical_and(me >= low, me < low + holders)
 
     @pl.when(holds)
     def _():

time: 17.5 us -> 17.2 us (0.983)
  Pallas kernels: 16.7 us -> 16.3 us
    pallas_call x1, Pallas kernels: 16.7 us -> 16.3 us  [on_device(): pl.pallas_call(functools.partial(kernel, n), out_shape=pltpu.VMEM((pairs,...]
where the time goes in v5:
time: 17.2 us; the launch traced here: 17 us
  Pallas kernels  16.3 us (95%)
  local copies, waits for them, and re-layouts  0.66 us (4%)
    pallas_call x1, Pallas kernels, on_device(): pl.pallas_call(functools.partial(kernel, n), out_shape=pltpu.VMEM((pairs,...  16.3 us
    unnamed x1, local copies, waits for them, and re-layouts  0.66 us

profile of v5, /device:TPU:0, one launch (start us, length us, event | category | flops | bytes accessed | tf_op | source)
XLA Modules:
  0.0 17.0 jit_solution(4077933057805888400)
XLA Ops:
  0.0 16.3 %shard_map.73 = bf16[64,8,128]{2,1,0:T(8,128)(2,1)S(1)} custom-call(bf16[64,8,128]{2,1,0:T(8,128)(2,1)} %bitcast.9, bf16[64,256,128]{2,1,0:T(8,128)(2,1)} %bitcast.7, bf16[64,256,128]{2,1,0:T(8,128)(2,1)} %bitcast.8, f32[2,16,32]{2,1,0:T(8,128)} %gate_ref.1, s32[16]{0:T(128)} %len_ref.1, s32[4,2,16]{2,1,0:T(2,128)} %bitcast.10, s32[4,16]{1,0:T(4,128)} %bitcast.11), custom_call_target="tpu_custom_call" | custom-call | tf_op jit(solution)/shard_map/pallas_call | solution.py:308
  16.3 0.7 %copy.9 = bf16[16,32,128]{2,1,0:T(8,128)(2,1)} copy(bf16[16,32,128]{2,1,0:T(8,128)(2,1)S(1)} %bitcast.6) | data formatting | bytes 262144
